TPU v7x, 32 devices: a whole 2x2x4 slice. The times are simulated.
32 devices in a mesh: seq: 8 (over y, x, core), head: 4 (over z).
Axes of the slice: x: 2, y: 2, z: 4, core: 2. Of those that a mesh axis runs over, the one named last changes fastest.
Arguments:
- tokens: bfloat16 [512, 4096], P('seq'), may hold values from -6 to 6
- norm_gain: bfloat16 [4096], replicated, may hold values from 0.25 to 1.75
- w_query: bfloat16 [4096, 4096], P(None, 'head'), may hold values from -0.09375 to 0.09375
- key_projection: bfloat16 [4096, 1024], P(None, 'head'), may hold values from -0.25 to 0.25
- value_projection: bfloat16 [4096, 1024], P(None, 'head'), may hold values from -0.09375 to 0.09375
- w_out: bfloat16 [4096, 4096], P('head'), may hold values from -0.09375 to 0.09375
- cache_keys: bfloat16 [8, 16384, 1024], P(None, 'seq', 'head'), may hold values from -60 to 60
- paged_value_cache: bfloat16 [8, 16384, 1024], P(None, 'seq', 'head'), may hold values from -6 to 6
- lengths: int32 [8], replicated, may hold values from 2048 to 16384
- parents: int32 [8, 64], replicated, may hold values from -1 to 62, as said below
- slot_block: int32 [8, 128], P(None, 'seq'), may hold values from 0 to 127, each once within a row
Outputs:
- mixed: bfloat16 [512, 4096], P('seq', 'head')
Inputs may be any that keep to these rules, and one draw needn't show every extreme that they name: parents[r, 0] = -1 for the root; for j >= 1, 0 <= parents[r, j] < j; the last token's parent is always token 62. Each row of slot_block is a permutation of 0 to 127.
All inputs are finite; a program needn't handle non-finite values.
Results may differ from a plain program's by a relative error of at most 0.0054.
The roundings to bfloat16 on the way count: a program that leaves them out, or rounds other values in their place, can miss the bound.
Values may be sent and summed in bfloat16 or wider, within the bound.
A program may use at most 128 MiB of HBM per device.

v0:
```python
import jax
import jax.numpy as jnp
from jax import lax
from jax.sharding import PartitionSpec as P

MODEL_WIDTH = 4096
HEAD_WIDTH = 128
TQ = 64
BLK = 128


norm_epsilon = 1e-05
masked_score = -1e30


def ancestors(parents):
    width_tree = parents.shape[-1]
    node_ids = jnp.arange(width_tree, dtype=jnp.int32)
    reached = (parents[..., :, None] == node_ids).astype(jnp.float32)
    reached = reached + (node_ids[:, None] == node_ids[None, :]).astype(jnp.float32)
    for repeat_step in range(max(1, (width_tree - 1).bit_length())):
        reached = jnp.minimum(
            jnp.einsum("rij,rjk->rik", reached, reached, precision=lax.Precision.HIGHEST), 1.0
        )
    return reached


def finish_group(group_max, group_total, group_sum):
    floored = jnp.maximum(group_total, 1.0)
    output = (group_sum / floored[..., None]).astype(jnp.bfloat16)
    return (output, group_max + jnp.log(floored))


def per_device(
    tokens,
    norm_gain,
    w_query,
    key_projection,
    value_projection,
    w_out,
    cache_keys,
    paged_value_cache,
    lengths,
    parents,
    slot_block,
):
    inputs = tokens.astype(jnp.float32)
    normed = (
        inputs
        * lax.rsqrt(jnp.mean(inputs * inputs, axis=-1, keepdims=True) + norm_epsilon)
        * norm_gain.astype(jnp.float32)
    ).astype(jnp.bfloat16)
    queries = jnp.dot(normed, w_query, preferred_element_type=jnp.float32).astype(jnp.bfloat16)
    key_new = jnp.dot(normed, key_projection, preferred_element_type=jnp.float32).astype(
        jnp.bfloat16
    )
    value_new = jnp.dot(normed, value_projection, preferred_element_type=jnp.float32).astype(
        jnp.bfloat16
    )
    local_rows = tokens.shape[0]
    kv_heads = key_projection.shape[1] // HEAD_WIDTH
    groups = w_query.shape[1] // key_projection.shape[1]
    local_context = cache_keys.shape[1]
    requests = lengths.shape[0]
    all_rows = requests * TQ
    score_scale = HEAD_WIDTH ** (-0.5)
    row_start = lax.axis_index("seq") * local_rows
    all_queries, all_keys, all_values = (
        lax.all_gather(queries, "seq", axis=0, tiled=True),
        lax.all_gather(key_new, "seq", axis=0, tiled=True),
        lax.all_gather(value_new, "seq", axis=0, tiled=True),
    )
    block_offsets = jnp.arange(BLK, dtype=jnp.int32)
    positions = (slot_block[:, :, None] * BLK + block_offsets[None, None, :]).reshape(
        requests, local_context
    )
    visible = (positions < lengths[:, None])[:, None, None, None, :]
    query_blocks = all_queries.reshape(requests, TQ, kv_heads, groups, HEAD_WIDTH)
    key_blocks = cache_keys.reshape(requests, local_context, kv_heads, HEAD_WIDTH)
    value_blocks = paged_value_cache.reshape(requests, local_context, kv_heads, HEAD_WIDTH)
    cache_scores = (
        jnp.einsum(
            "rthgd,rchd->rthgc", query_blocks, key_blocks, preferred_element_type=jnp.float32
        )
        * score_scale
    )
    cache_scores = jnp.where(visible, cache_scores, masked_score)
    cache_max = cache_scores.max(-1)
    cache_weights = jnp.where(visible, jnp.exp(cache_scores - cache_max[..., None]), 0.0)
    cache_total = cache_weights.sum(-1).reshape(all_rows, kv_heads, groups)
    cache_sum = jnp.einsum(
        "rthgc,rchd->rthgd",
        cache_weights.astype(jnp.bfloat16),
        value_blocks,
        preferred_element_type=jnp.float32,
    )
    cache_sum = cache_sum.reshape(all_rows, kv_heads, groups, HEAD_WIDTH)
    cache_max = cache_max.reshape(all_rows, kv_heads, groups)
    cache_out, cache_lse = finish_group(cache_max, cache_total, cache_sum)
    window = max(local_rows, TQ)
    window_start = row_start // window * window
    row_ids = row_start + jnp.arange(local_rows, dtype=jnp.int32)
    row_request = row_ids // TQ
    key_request = (window_start + jnp.arange(window, dtype=jnp.int32)) // TQ
    reached_rows = lax.dynamic_slice_in_dim(
        ancestors(parents).reshape(all_rows, TQ), row_start, local_rows, 0
    )
    tree_seen = (jnp.tile(reached_rows, (1, window // TQ)) > 0.5) & (
        key_request[None, :] == row_request[:, None]
    )
    tree_seen = tree_seen[:, None, None, :]
    own_queries = queries.reshape(local_rows, kv_heads, groups, HEAD_WIDTH)
    tree_keys = lax.dynamic_slice_in_dim(all_keys, window_start, window, 0).reshape(
        window, kv_heads, HEAD_WIDTH
    )
    tree_values = lax.dynamic_slice_in_dim(all_values, window_start, window, 0).reshape(
        window, kv_heads, HEAD_WIDTH
    )
    tree_scores = (
        jnp.einsum("thgd,uhd->thgu", own_queries, tree_keys, preferred_element_type=jnp.float32)
        * score_scale
    )
    tree_scores = jnp.where(tree_seen, tree_scores, masked_score)
    tree_max = tree_scores.max(-1)
    tree_weights = jnp.where(tree_seen, jnp.exp(tree_scores - tree_max[..., None]), 0.0)
    tree_total = tree_weights.sum(-1)
    tree_sum = jnp.einsum(
        "thgu,uhd->thgd",
        tree_weights.astype(jnp.bfloat16),
        tree_values,
        preferred_element_type=jnp.float32,
    )
    tree_out, tree_lse = finish_group(tree_max, tree_total, tree_sum)
    seq_count = lax.axis_size("seq")
    peer_out = lax.all_to_all(cache_out, "seq", split_axis=0, concat_axis=0, tiled=True)
    peer_lse = lax.all_to_all(cache_lse, "seq", split_axis=0, concat_axis=0, tiled=True)
    peer_out = peer_out.reshape(seq_count, local_rows, kv_heads, groups, HEAD_WIDTH)
    peer_lse = peer_lse.reshape(seq_count, local_rows, kv_heads, groups)
    best = jnp.maximum(peer_lse.max(0), tree_lse)
    peer_factor = jnp.exp(peer_lse - best[None])
    tree_factor = jnp.exp(tree_lse - best)
    own_sum = (
        jnp.einsum("nthg,nthgd->thgd", peer_factor, peer_out.astype(jnp.float32))
        + tree_out.astype(jnp.float32) * tree_factor[..., None]
    )
    own_total = peer_factor.sum(0) + tree_factor
    attended = (own_sum / own_total[..., None]).astype(jnp.bfloat16).reshape(local_rows, -1)
    own_width = MODEL_WIDTH // lax.axis_size("head")
    reduced = lax.psum_scatter(
        jnp.einsum("kc,tk->ct", w_out, attended, preferred_element_type=jnp.float32),
        "head",
        scatter_dimension=0,
        tiled=True,
    )
    residual = lax.dynamic_slice_in_dim(inputs, lax.axis_index("head") * own_width, own_width, 1)
    return (residual + reduced.T).astype(jnp.bfloat16)


def solution(mesh):
    in_specs = (
        P("seq", None),
        P(),
        P(None, "head"),
        P(None, "head"),
        P(None, "head"),
        P("head", None),
        P(None, "seq", "head"),
        P(None, "seq", "head"),
        P(),
        P(),
        P(None, "seq"),
    )
    out_specs = P("seq", "head")
    return jax.shard_map(
        per_device, mesh=mesh, in_specs=in_specs, out_specs=out_specs, check_vma=False
    )
```

profile of v0, /device:TPU:0, one launch (start us, length us, event | category | flops | bytes accessed | tf_op | source)
XLA Modules:
  0.0 192.5 jit_solution(16187131166753318771)
XLA Ops:
  6.5 0.0 copy-start
  6.5 0.0 all-gather.2.cloned.1.call-start
  6.5 0.8 convert_element_type.51
  7.4 1.2 multiply_reduce_fusion
  8.6 0.0 copy-start.3
  8.7 0.0 copy-start.2
  8.7 5.9 %convolution_convert_fusion = bf16[64,1024]{1,0:T(8,128)(2,1)} fusion(bf16[4096,1024]{1,0:T(8,128)(2,1)} %param.13, f32[4096]{0:T(1024)S(1)} %convert_element_type.51, f32[64]{0:T(128)S(1)} %add_rsqrt_fusion, bf16[64,4096]{1,0:T(8,128)(2,1)} %param.11), kind=kOutput, calls=%fused_computation.33 | convolution fusion | flops 537985024 | bytes 9060608 | tf_op jit(solution)/shard_map/dot_general | solution.py:53
  14.6 0.0 all-gather.2.cloned.1.call-update
  14.7 0.5 convolution_minimum_fusion.5
  15.2 0.4 convolution_minimum_fusion.4
  15.6 0.4 convolution_minimum_fusion.3
  16.0 0.4 convolution_minimum_fusion.2
  16.4 0.4 convolution_minimum_fusion.1
  16.7 0.4 convolution_minimum_fusion
  17.1 0.1 fusion.47
  17.2 1.0 reshape.182
  18.2 0.1 copy.110
  18.3 0.5 convolution_convert_fusion.2
  18.9 11.1 %all_gather.10 = bf16[512,256]{1,0:T(8,128)(2,1)S(1)} all-gather(bf16[64,256]{1,0:T(8,128)(2,1)S(1)} %convolution_convert_fusion.2), channel_id=1, replica_groups=mesh['seq'=8,'head'=4] {'seq'}, dimensions={0}, use_global_device_ids=true | all-gather | bytes 294912 | tf_op jit(solution)/shard_map/all_gather | solution.py:70
  30.0 2.1 %convolution_convert_fusion.1 = bf16[64,256]{1,0:T(8,128)(2,1)S(1)} fusion(bf16[4096,256]{1,0:T(8,128)(2,1)} %param.15, f32[4096]{0:T(1024)S(1)} %convert_element_type.51, f32[64]{0:T(128)S(1)} %add_rsqrt_fusion, bf16[64,4096]{1,0:T(8,128)(2,1)S(1)} %copy-done.2), kind=kOutput, calls=%fused_computation.35 | convolution fusion | flops 135282688 | bytes 2670848 | tf_op jit(solution)/shard_map/dot_general | solution.py:57
  32.1 9.6 %all_gather.11 = bf16[512,256]{1,0:T(8,128)(2,1)S(1)} all-gather(bf16[64,256]{1,0:T(8,128)(2,1)S(1)} %convolution_convert_fusion.1), channel_id=1, replica_groups=mesh['seq'=8,'head'=4] {'seq'}, dimensions={0}, use_global_device_ids=true | all-gather | bytes 294912 | tf_op jit(solution)/shard_map/all_gather | solution.py:71
  41.8 0.1 copy.104
  41.9 12.5 %reshape.177 = bf16[8,2048,2,128]{3,2,1,0:T(2,128)(2,1)} reshape(bf16[8,2048,256]{2,1,0:T(8,128)(2,1)} %param.17) | data formatting | bytes 16777216 | tf_op jit(solution)/shard_map/reshape | solution.py:79
  54.4 12.5 %reshape.183 = bf16[8,2048,2,128]{3,2,1,0:T(2,128)(2,1)} reshape(bf16[8,2048,256]{2,1,0:T(8,128)(2,1)} %param.18) | data formatting | bytes 16777216 | tf_op jit(solution)/shard_map/reshape | solution.py:80
  66.9 0.3 fusion.54
  67.2 0.1 fusion.43
  67.3 0.0 all-gather.2.cloned.1.call-done
  67.3 1.8 reshape.176
  69.1 17.5 %bitcast_reduce_fusion = (f32[8,64,2,4]{1,3,2,0:T(4,128)S(1)}, f32[8,2,64,4,2048]{4,2,3,1,0:T(8,128)}) fusion(pred[8,2048]{1,0:T(8,128)(4,1)S(1)} %fusion.43, bf16[8,2048,2,128,1]{3,2,1,0,4:T(2,128)(2,1)} %bitcast.91, bf16[8,64,2,4,128]{4,3,2,1,0:T(4,128)(2,1)S(1)} %reshape.176), kind=kOutput, calls=%fused_computation.1 | convolution fusion | flops 2172645376 | bytes 43024384 | tf_op jit(solution)/shard_map/rthgd,rchd->rthgc/dot_general | solution.py:82
  86.6 15.1 %fusion.3 = f32[8,64,2,4]{1,3,2,0:T(4,128)S(1)} fusion(f32[8,2,64,4,2048]{4,2,3,1,0:T(8,128)} %get-tuple-element.12, f32[8,64,2,4]{1,3,2,0:T(4,128)S(1)} %get-tuple-element.11, pred[8,2048]{1,0:T(8,128)(4,1)S(1)} %fusion.43), kind=kLoop, calls=%fused_computation.6 | loop fusion | flops 41938944 | bytes 33603584 | tf_op jit(solution)/shard_map/reduce_sum | solution.py:90
  101.7 0.1 max.49
  101.8 0.1 reshape.178
  101.9 0.3 copy.109
  102.1 1.3 reshape.194
  103.5 3.5 %all-to-all-start = ((f32[8,1,512]{2,1,0:T(1,128)}), f32[8,1,512]{2,1,0:T(1,128)S(1)}, u32[]{:S(2)}, u32[]{:S(2)}) async-start(f32[8,1,512]{2,1,0:T(1,128)} %reshape.194), calls=%async_computation | async-start | bytes 32768 | tf_op jit(solution)/shard_map/all_to_all | solution.py:136
  107.0 18.7 %fusion.12 = f32[8,64,2,4,128]{4,1,3,2,0:T(8,128)} fusion(bf16[8,2048,2,128,1]{3,2,1,0,4:T(2,128)(2,1)} %bitcast.92, f32[8,2,64,4,2048]{4,2,3,1,0:T(8,128)} %get-tuple-element.12, f32[8,64,2,4]{1,3,2,0:T(4,128)S(1)} %get-tuple-element.11, pred[8,2048]{1,0:T(8,128)(4,1)S(1)} %fusion.43), kind=kOutput, calls=%fused_computation.16 | convolution fusion | flops 2189426688 | bytes 44072960 | tf_op jit(solution)/shard_map/rthgc,rchd->rthgd/dot_general | solution.py:91
  125.7 1.8 copy.116
  127.5 0.9 fusion.11
  128.4 1.8 copy.117
  130.2 0.0 all-to-all-done
  130.2 4.1 %all-to-all-start.1 = ((bf16[512,2,4,128]{3,2,1,0:T(4,128)(2,1)}), bf16[512,2,4,128]{3,2,1,0:T(4,128)(2,1)S(1)}, u32[]{:S(2)}, u32[]{:S(2)}) async-start(bf16[512,2,4,128]{3,2,1,0:T(4,128)(2,1)} %copy.117), calls=%async_computation.1 | async-start | bytes 2097152 | tf_op jit(solution)/shard_map/all_to_all | solution.py:135
  134.3 0.0 reduce-scatter.2.cloned.1.call-start
  134.4 0.1 fusion.35
  134.5 0.5 broadcast.150
  135.0 0.7 reduce
  135.7 0.8 reshape.195
  136.5 0.3 reduce_max.28
  136.8 0.1 copy.113
  136.9 0.1 copy.114
  137.0 0.4 fusion.29
  137.5 0.1 copy.120
  137.6 0.3 fusion.30
  137.9 1.7 copy.125
  139.6 10.1 %all-to-all-done.1 = bf16[512,2,4,128]{3,2,1,0:T(4,128)(2,1)S(1)} async-done(((bf16[512,2,4,128]{3,2,1,0:T(4,128)(2,1)}), bf16[512,2,4,128]{3,2,1,0:T(4,128)(2,1)S(1)}, u32[]{:S(2)}, u32[]{:S(2)}) %all-to-all-start.1) | async-done | bytes 1048608 | tf_op jit(solution)/shard_map/all_to_all | solution.py:135
  149.7 0.9 fusion.27
  150.6 0.4 fusion.25
  151.0 0.1 copy.121
  151.1 0.0 copy-start.1
  151.1 0.1 reshape.187
  151.2 6.1 %convolution_bitcast_fusion = f32[4096,64]{0,1:T(8,128)} fusion(bf16[64,1024]{1,0:T(8,128)(2,1)S(1)} %reshape.187, bf16[1024,4096]{1,0:T(8,128)(2,1)} %param.16), kind=kOutput, calls=%fused_computation.13 | convolution fusion | flops 536870912 | bytes 9568256 | tf_op jit(solution)/shard_map/kc,tk->ct/dot_general | solution.py:150
  157.2 0.0 reduce-scatter.2.cloned.1.call-update
  157.3 1.1 convert_element_type.50
  158.4 25.5 %reduce-scatter.2.cloned.1.call-done = f32[1024,64]{0,1:T(8,128)} async-done(((f32[4096,64]{0,1:T(8,128)}), f32[1024,64]{0,1:T(8,128)}) %reduce-scatter.2.cloned.1.call-update) | async-done | bytes 262160 | tf_op jit(solution)/shard_map/reduce_scatter | solution.py:149
  183.9 1.7 fusion.31
  (21 shorter events, 0.1 us)
Async XLA Ops:
  6.5 11.8 %copy-start = (bf16[4096,256]{1,0:T(8,128)(2,1)S(1)}, bf16[4096,256]{1,0:T(8,128)(2,1)}, u32[]{:S(2)}) copy-start(bf16[4096,256]{1,0:T(8,128)(2,1)} %param.14) | copy-start | bytes 6291460
  6.5 60.8 %all-gather.2.cloned.1.call-start = ((), (), s32[]{:S(2)}) async-start(), calls=%async_computation.3 | async-start | bytes 1179648 | tf_op jit(solution)/shard_map/all_gather | solution.py:69
  8.6 6.0 %copy-start.3 = (s32[8,64]{1,0:T(8,128)S(1)}, s32[8,64]{1,0:T(8,128)}, u32[]{:S(2)}) copy-start(s32[8,64]{1,0:T(8,128)} %param.20) | copy-start | bytes 6148
  8.7 9.7 %copy-start.2 = (bf16[64,4096]{1,0:T(8,128)(2,1)S(1)}, bf16[64,4096]{1,0:T(8,128)(2,1)}, u32[]{:S(2)}) copy-start(bf16[64,4096]{1,0:T(8,128)(2,1)} %param.11) | copy-start | bytes 1572868
  14.6 27.2 %copy-start.4 = (s32[8,16]{1,0:T(8,128)S(1)}, s32[8,16]{1,0:T(8,128)}, u32[]{:S(2)}) copy-start(s32[8,16]{1,0:T(8,128)} %param.21) | copy-start | bytes 1540
  54.4 12.8 %copy-start.5 = (s32[8]{0:T(128)S(1)}, s32[8]{0:T(128)}, u32[]{:S(2)}) copy-start(s32[8]{0:T(128)} %param.19) | copy-start | bytes 100
  103.5 26.7 %all-to-all-start = ((f32[8,1,512]{2,1,0:T(1,128)}), f32[8,1,512]{2,1,0:T(1,128)S(1)}, u32[]{:S(2)}, u32[]{:S(2)}) async-start(f32[8,1,512]{2,1,0:T(1,128)} %reshape.194), calls=%async_computation | async-start | bytes 32768 | tf_op jit(solution)/shard_map/all_to_all | solution.py:136
  130.2 19.5 %all-to-all-start.1 = ((bf16[512,2,4,128]{3,2,1,0:T(4,128)(2,1)}), bf16[512,2,4,128]{3,2,1,0:T(4,128)(2,1)S(1)}, u32[]{:S(2)}, u32[]{:S(2)}) async-start(bf16[512,2,4,128]{3,2,1,0:T(4,128)(2,1)} %copy.117), calls=%async_computation.1 | async-start | bytes 2097152 | tf_op jit(solution)/shard_map/all_to_all | solution.py:135
  134.3 49.6 %reduce-scatter.2.cloned.1.call-start = ((), (), s32[]{:S(2)}) async-start(), calls=%async_computation.4 | async-start | bytes 1310720 | tf_op jit(solution)/shard_map/reduce_scatter | solution.py:149
  151.1 34.5 %copy-start.1 = (bf16[4096,256]{1,0:T(8,128)(2,1)S(1)}, bf16[4096,256]{1,0:T(8,128)(2,1)}, u32[]{:S(2)}) copy-start(bf16[4096,256]{1,0:T(8,128)(2,1)} %param.14) | copy-start | bytes 6291460
Sparse Core Ops, SparseCore 0:
  14.7 26.7 all-gather.1
  157.4 26.4 reduce-scatter.1
where the time goes:
time: 194 us; the launch traced here: 192 us
  matrix products  54.7 us (28%)
  local copies, waits for them, and re-layouts  37 us (19%)
  waiting for transfers between devices  35.6 us (18%)
  other arithmetic  22.9 us (12%)
  blocking collectives  20.8 us (11%)
  between operations  13.8 us (7%)
  starting transfers between devices  7.67 us (4%)
    reduce_scatter x1, waiting for transfers between devices, per_device(): lax.psum_scatter(jnp.einsum('kc,tk->ct', w_out, attended, preferred_eleme...  25.5 us
    dot_general x1, matrix products, per_device(): jnp.einsum('rthgc,rchd->rthgd', cache_weights.astype(jnp.bfloat16), value...  18.7 us
    dot_general x1, matrix products, per_device(): jnp.einsum('rthgd,rchd->rthgc', query_blocks, key_blocks, preferred_eleme...  17.5 us
    reduce_sum x1, other arithmetic, per_device(): cache_total = cache_weights.sum(-1).reshape(all_rows, kv_heads, groups)  15.1 us
    reshape x1, local copies, waits for them, and re-layouts, per_device(): paged_value_cache.reshape(requests, local_context, kv_heads, HEAD_WIDTH)  12.5 us
    reshape x1, local copies, waits for them, and re-layouts, per_device(): cache_keys.reshape(requests, local_context, kv_heads, HEAD_WIDTH)  12.5 us
    all_gather x1, blocking collectives, per_device(): lax.all_gather(key_new, 'seq', axis=0, tiled=True)  11.1 us
    all_to_all x1, waiting for transfers between devices, per_device(): lax.all_to_all(cache_out, 'seq', split_axis=0, concat_axis=0, tiled=True)  10.1 us
  transfers between devices with their start and end apart: 4, of which 2 were waited for; matrix products, arithmetic and copies ran while one was open for 32% of the time, Pallas kernels for 0%

commit v1 on v0

v1 whole, which is shorter than its diff:
```python
import functools

import jax
import jax.numpy as jnp
from jax import lax
from jax.experimental import pallas as pl
from jax.experimental.pallas import tpu as pltpu
from jax.sharding import PartitionSpec as P

HEAD_WIDTH = 128
TQ = 64
BLK = 128

norm_epsilon = 1e-05
masked_score = -1e30
MESH = pl.DeviceIdType.MESH
f32 = jnp.float32
bf16 = jnp.bfloat16


def xor(a, b, count):
    out, bit = 0, 1
    while bit < count:
        p, q = (a // bit) % 2, (b // bit) % 2
        out = out + bit * (p + q - 2 * p * q)
        bit *= 2
    return out


def columns_to_rows(cols, pad_rows):
    n = cols[0].shape[0]
    lane = lax.broadcasted_iota(jnp.int32, (n, 128), 1)
    tile = jnp.zeros((n, 128), f32)
    for index, col in enumerate(cols):
        tile = jnp.where(lane == index, col, tile)
    if n < 128:
        tile = jnp.concatenate([tile, jnp.zeros((128 - n, 128), f32)], axis=0)
    return tile.T[:pad_rows]


def kernel(
    dims,
    len_ref,
    slot_ref,
    parents_ref,
    gain_ref,
    tok_hbm,
    wq_hbm,
    wk_hbm,
    wv_hbm,
    wo_hbm,
    k_hbm,
    v_hbm,
    out_ref,
    tok,
    wq,
    wkv,
    wo,
    kbuf,
    vbuf,
    q_all,
    kv_own,
    reach_ref,
    bias,
    osend,
    orecv,
    lsend,
    lrecv,
    tree_out,
    att,
    zsend,
    zrecv,
    tok_sem,
    wq_sem,
    wkv_sem,
    wo_sem,
    k_sem,
    v_sem,
    q_send,
    q_recv,
    f_send,
    o_send,
    o_recv,
    l_send,
    l_recv,
    t_send,
    t_recv,
    z_send,
    z_recv,
):
    S, H, R, LR, KVH, G, LC = dims
    D = HEAD_WIDTH
    GD = G * D
    HG = KVH * G
    HGP = lsend.shape[1]
    nch = S // 2
    group = TQ // LR
    scale = D**-0.5
    exp2_scale = scale * 1.4426950408889634
    me = lax.axis_index("seq")
    mh = lax.axis_index("head")
    chip, core = me // 2, me % 2
    partner = chip * 2 + (1 - core)
    W = out_ref.shape[1]

    def remote(src, dst, ssem, rsem, seq=None, head=None):
        return pltpu.make_async_remote_copy(
            src_ref=src,
            dst_ref=dst,
            send_sem=ssem,
            recv_sem=rsem,
            device_id=(me if seq is None else seq, mh if head is None else head),
            device_id_type=MESH,
        )

    def device_at(i):
        same = xor(chip, i - 1, nch) * 2 + core
        other = xor(chip, 2 * nch - i, nch) * 2 + (1 - core)
        dev = jnp.where(i <= nch, same, other)
        dev = jnp.where(i == 1, partner, dev)
        return jnp.where(i == 0, me, dev)

    tok_copy = pltpu.make_async_copy(tok_hbm, tok, tok_sem)
    tok_copy.start()
    wq_copies = []
    for c in range(KVH):
        wq_copies.append(
            pltpu.make_async_copy(wq_hbm.at[:, c * GD : (c + 1) * GD], wq.at[c], wq_sem.at[c])
        )
        wq_copies[-1].start()
    wkv_copies = [
        pltpu.make_async_copy(wk_hbm, wkv.at[0], wkv_sem.at[0]),
        pltpu.make_async_copy(wv_hbm, wkv.at[1], wkv_sem.at[1]),
    ]
    for copy in wkv_copies:
        copy.start()

    barrier = pltpu.get_barrier_semaphore()
    for j in range(1, S):
        pl.semaphore_signal(barrier, inc=1, device_id=((me + j) % S, mh), device_id_type=MESH)
    for j in range(1, H):
        pl.semaphore_signal(barrier, inc=1, device_id=(me, (mh + j) % H), device_id_type=MESH)

    row_ids = lax.broadcasted_iota(jnp.int32, (TQ, TQ), 0)
    col_ids = lax.broadcasted_iota(jnp.int32, (TQ, TQ), 1)
    eye = row_ids == col_ids
    own_request = me // group
    parents_row = parents_ref[pl.ds(own_request, 1), :].astype(f32)
    parent_col = jnp.sum(jnp.where(eye, parents_row, 0.0), axis=1, keepdims=True)
    reached = ((parent_col == col_ids.astype(f32)) | eye).astype(f32)
    for _ in range(max(1, (TQ - 1).bit_length())):
        step = reached.astype(bf16)
        reached = jnp.minimum(jnp.dot(step, step, preferred_element_type=f32), 1.0)
    reach_ref[...] = reached

    lane = lax.broadcasted_iota(jnp.int32, (1, BLK), 1)
    for r in range(R):
        for b in range(LC // BLK):
            shown = slot_ref[r, b] * BLK + lane < len_ref[r]
            bias[r, :, b * BLK : (b + 1) * BLK] = jnp.where(shown, 0.0, masked_score)

    tok_copy.wait()
    inputs = tok[...].astype(f32)
    normed = (
        inputs
        * lax.rsqrt(jnp.mean(inputs * inputs, axis=-1, keepdims=True) + norm_epsilon)
        * gain_ref[...].astype(f32)
    ).astype(bf16)

    for c in range(KVH):
        wq_copies[c].wait()
        q_all[me, c] = jnp.dot(normed, wq[c], preferred_element_type=f32).astype(bf16)
        if c == 0:
            def load(i, carry):
                r = device_at(i) if group == 1 else i
                pltpu.make_async_copy(k_hbm.at[r], kbuf.at[r], k_sem.at[r]).start()
                pltpu.make_async_copy(v_hbm.at[r], vbuf.at[r], v_sem.at[r]).start()
                return carry

            lax.fori_loop(0, R, load, 0)
            for h in range(H):
                pltpu.make_async_copy(
                    wo_hbm.at[:, h * W : (h + 1) * W], wo.at[h], wo_sem.at[h]
                ).start()

    pl.semaphore_wait(barrier, S - 1 + H - 1)
    q_copies = []
    for i in range(1, nch + 1):
        to = partner if i == 1 else xor(chip, i - 1, nch) * 2 + core
        q_copies.append(
            remote(q_all.at[me], q_all.at[me], q_send.at[i], q_recv.at[me], seq=to)
        )
        q_copies[-1].start()

    slot = me % group
    for which in range(2):
        wkv_copies[which].wait()
        kv_own[slot, which] = jnp.dot(normed, wkv[which], preferred_element_type=f32).astype(bf16)
    base = own_request * group
    kv_copies = []
    for j in range(1, group):
        kv_copies.append(
            remote(
                kv_own.at[slot],
                kv_own.at[slot],
                t_send.at[j],
                t_recv.at[slot],
                seq=base + (slot + j) % group,
            )
        )
        kv_copies[-1].start()
    for j in range(1, group):
        source = (slot + j) % group
        remote(kv_own.at[source], kv_own.at[source], t_send.at[j], t_recv.at[source]).wait_recv()
    for copy in kv_copies:
        copy.wait_send()

    def stacked(block):
        return jnp.concatenate([block[:, g * D : (g + 1) * D] for g in range(G)], axis=0)

    seen = reach_ref[pl.ds(pl.multiple_of(slot * LR, LR), LR), :] > 0.5
    tree_cols = []
    for h in range(KVH):
        keys = jnp.concatenate([kv_own[s, 0, :, h * D : (h + 1) * D] for s in range(group)], axis=0)
        vals = jnp.concatenate([kv_own[s, 1, :, h * D : (h + 1) * D] for s in range(group)], axis=0)
        for g in range(G):
            q = q_all[me, h, :, g * D : (g + 1) * D]
            s = lax.dot_general(q, keys, (((1,), (1,)), ((), ())), preferred_element_type=f32)
            s = jnp.where(seen, s * scale, masked_score)
            m = jnp.max(s, axis=-1, keepdims=True)
            p = jnp.where(seen, jnp.exp(s - m), 0.0)
            total = jnp.maximum(jnp.sum(p, axis=-1, keepdims=True), 1.0)
            o = jnp.dot(p.astype(bf16), vals, preferred_element_type=f32)
            at = (h * G + g) * D
            tree_out[:, at : at + D] = (o / total).astype(bf16)
            tree_cols.append(m + jnp.log(total))
    tree_lse = columns_to_rows(tree_cols, HGP)

    if group > 1:
        for r in range(R):
            pltpu.make_async_copy(k_hbm.at[r], kbuf.at[r], k_sem.at[r]).wait()
            pltpu.make_async_copy(v_hbm.at[r], vbuf.at[r], v_sem.at[r]).wait()

    def attend(i, carry):
        dev = device_at(i)
        r = dev // group

        @pl.when(i > 0)
        def _():
            remote(q_all.at[dev], q_all.at[dev], q_send.at[0], q_recv.at[dev]).wait_recv()

        @pl.when((i > 1) & (i <= nch))
        def _():
            remote(
                q_all.at[dev], q_all.at[dev], f_send.at[i], q_recv.at[dev], seq=partner
            ).start()

        if group == 1:
            pltpu.make_async_copy(k_hbm.at[r], kbuf.at[r], k_sem.at[r]).wait()
            pltpu.make_async_copy(v_hbm.at[r], vbuf.at[r], v_sem.at[r]).wait()
        hidden = bias[r]
        cols = []
        for h in range(KVH):
            q = stacked(q_all[dev, h])
            keys = kbuf[r, :, h * D : (h + 1) * D]
            vals = vbuf[r, :, h * D : (h + 1) * D]
            s = lax.dot_general(q, keys, (((1,), (1,)), ((), ())), preferred_element_type=f32)
            s = s + hidden
            m = jnp.max(s, axis=-1, keepdims=True)
            p = jnp.exp2((s - m) * exp2_scale)
            total = jnp.maximum(jnp.sum(p, axis=-1, keepdims=True), 1.0)
            o = jnp.dot(p.astype(bf16), vals, preferred_element_type=f32)
            o = (o / total).astype(bf16)
            lse = m * scale + jnp.log(total)
            for g in range(G):
                at = (h * G + g) * D
                osend[dev, :, at : at + D] = o[g * LR : (g + 1) * LR]
                cols.append(lse[g * LR : (g + 1) * LR])
        lsend[dev] = columns_to_rows(cols, HGP)

        @pl.when(i > 0)
        def _():
            remote(osend.at[dev], orecv.at[me], o_send.at[i], o_recv.at[me], seq=dev).start()
            remote(lsend.at[dev], lrecv.at[me], l_send.at[i], l_recv.at[me], seq=dev).start()

        return carry

    lax.fori_loop(0, S, attend, 0)

    for copy in q_copies:
        copy.wait_send()
    for i in range(2, nch + 1):
        remote(q_all.at[me], q_all.at[me], f_send.at[i], q_recv.at[me]).wait_send()
    orecv[me] = osend[me]
    lrecv[me] = lsend[me]

    def arrive(i, carry):
        dev = device_at(i)
        remote(osend.at[dev], orecv.at[dev], o_send.at[i], o_recv.at[dev]).wait()
        remote(lsend.at[dev], lrecv.at[dev], l_send.at[i], l_recv.at[dev]).wait()
        return carry

    lax.fori_loop(1, S, arrive, 0)

    lse = [lrecv[s] for s in range(S)] + [tree_lse]
    best = functools.reduce(jnp.maximum, lse)
    factors = [jnp.exp(x - best) for x in lse]
    whole = functools.reduce(jnp.add, factors)
    rows = jnp.concatenate([x / whole for x in factors], axis=0)
    pad = -rows.shape[0] % 128
    if pad:
        rows = jnp.concatenate([rows, jnp.zeros((pad, 128), f32)], axis=0)
    weights = rows.T[:LR]
    for n in range(HG):
        at = n * D
        col = S * HGP + n
        total = weights[:, col : col + 1] * tree_out[:, at : at + D].astype(f32)
        for s in range(S):
            col = s * HGP + n
            total = total + weights[:, col : col + 1] * orecv[s, :, at : at + D].astype(f32)
        att[:, at : at + D] = total.astype(bf16)

    for h in range(H):
        pltpu.make_async_copy(wo_hbm.at[:, h * W : (h + 1) * W], wo.at[h], wo_sem.at[h]).wait()
    attended = att[...]
    order = sorted(range(1, H), key=lambda j: -min(j, H - j))
    z_copies = []
    for j in order:
        to = (mh + j) % H
        zsend[j] = jnp.dot(attended, wo[to], preferred_element_type=f32).astype(bf16)
        z_copies.append(
            remote(zsend.at[j], zrecv.at[mh], z_send.at[j], z_recv.at[mh], head=to)
        )
        z_copies[-1].start()
    mixed = jnp.dot(attended, wo[mh], preferred_element_type=f32)
    mixed = mixed + tok[:, pl.ds(pl.multiple_of(mh * W, W), W)].astype(f32)
    for j in order:
        source = (mh + H - j) % H
        remote(zsend.at[j], zrecv.at[source], z_send.at[j], z_recv.at[source]).wait_recv()
        mixed = mixed + zrecv[source].astype(f32)
    out_ref[...] = mixed.astype(bf16)
    for copy in z_copies:
        copy.wait_send()


def solution(mesh):
    S, H = mesh.shape["seq"], mesh.shape["head"]

    def per_device(
        tokens, norm_gain, w_query, key_projection, value_projection, w_out,
        cache_keys, paged_value_cache, lengths, parents, slot_block,
    ):
        LR, M = tokens.shape
        D = HEAD_WIDTH
        KVH = key_projection.shape[1] // D
        G = w_query.shape[1] // key_projection.shape[1]
        R, LC = cache_keys.shape[:2]
        W = w_out.shape[1] // H
        HG = KVH * G
        HGP = -(-HG // 8) * 8
        group = TQ // LR
        dma = pltpu.SemaphoreType.DMA
        vmem = pl.BlockSpec(memory_space=pltpu.VMEM)
        smem = pl.BlockSpec(memory_space=pltpu.SMEM)
        hbm = pl.BlockSpec(memory_space=pl.ANY)
        return pl.pallas_call(
            functools.partial(kernel, (S, H, R, LR, KVH, G, LC)),
            out_shape=jax.ShapeDtypeStruct((LR, W), bf16),
            in_specs=[smem, smem, vmem, vmem] + [hbm] * 7,
            out_specs=vmem,
            scratch_shapes=[
                pltpu.VMEM((LR, M), bf16),
                pltpu.VMEM((KVH, M, G * D), bf16),
                pltpu.VMEM((2, M, KVH * D), bf16),
                pltpu.VMEM((H, HG * D, W), bf16),
                pltpu.VMEM((R, LC, KVH * D), bf16),
                pltpu.VMEM((R, LC, KVH * D), bf16),
                pltpu.VMEM((S, KVH, LR, G * D), bf16),
                pltpu.VMEM((group, 2, LR, KVH * D), bf16),
                pltpu.VMEM((TQ, TQ), f32),
                pltpu.VMEM((R, 1, LC), f32),
                pltpu.VMEM((S, LR, HG * D), bf16),
                pltpu.VMEM((S, LR, HG * D), bf16),
                pltpu.VMEM((S, HGP, 128), f32),
                pltpu.VMEM((S, HGP, 128), f32),
                pltpu.VMEM((LR, HG * D), bf16),
                pltpu.VMEM((LR, HG * D), bf16),
                pltpu.VMEM((H, LR, W), bf16),
                pltpu.VMEM((H, LR, W), bf16),
                dma,
                dma((KVH,)),
                dma((2,)),
                dma((H,)),
                dma((R,)),
                dma((R,)),
                dma((S,)),
                dma((S,)),
                dma((S,)),
                dma((S,)),
                dma((S,)),
                dma((S,)),
                dma((S,)),
                dma((group,)),
                dma((group,)),
                dma((H,)),
                dma((H,)),
            ],
            compiler_params=pltpu.CompilerParams(
                collective_id=0, has_side_effects=True, vmem_limit_bytes=66 * 1000 * 1000
            ),
        )(
            lengths, slot_block, parents, norm_gain.reshape(1, M), tokens,
            w_query, key_projection, value_projection, w_out, cache_keys, paged_value_cache,
        )

    in_specs = (
        P("seq", None),
        P(),
        P(None, "head"),
        P(None, "head"),
        P(None, "head"),
        P("head", None),
        P(None, "seq", "head"),
        P(None, "seq", "head"),
        P(),
        P(),
        P(None, "seq"),
    )
    return jax.shard_map(
        per_device, mesh=mesh, in_specs=in_specs, out_specs=P("seq", "head"), check_vma=False
    )
```

time: 194 us -> 50.9 us (0.26)
  matrix products: 54.7 us -> 0 us
  Pallas kernels: 0 us -> 47.7 us
  waiting for transfers between devices: 35.6 us -> 0 us
  local copies, waits for them, and re-layouts: 37 us -> 2.88 us
  other arithmetic: 22.9 us -> 0 us
  blocking collectives: 20.8 us -> 0 us
  between operations: 13.8 us -> 0.01 us
  starting transfers between devices: 7.67 us -> 0 us
    dot_general x15 -> x0, matrix products: 54.7 us -> none  [the longest x1 18.7 us: per_device(): jnp.einsum('rthgc,rchd->rthgd', cache_weights.astype(jnp.bfloat16), value...]
    pallas_call x0 -> x1, Pallas kernels: none -> 47.7 us  [per_device(): pl.pallas_call(functools.partial(kernel, (S, H, R, LR, KVH, G, LC)), out_...]
    reshape x8 -> x1, local copies, waits for them, and re-layouts: 28 us -> 1.31 us  [per_device(): norm_gain.reshape(1, M)]
    reduce_scatter x1 -> x0, waiting for transfers between devices: 25.5 us -> none  [per_device(): lax.psum_scatter(jnp.einsum('kc,tk->ct', w_out, attended, preferred_eleme...]
    all_gather x2 -> x0, blocking collectives: 20.8 us -> none  [the longest x1 11.1 us: per_device(): lax.all_gather(key_new, 'seq', axis=0, tiled=True)]
    reduce_sum x4 -> x0, other arithmetic: 16.8 us -> none  [the longest x1 15.1 us: per_device(): cache_total = cache_weights.sum(-1).reshape(all_rows, kv_heads, groups)]
    all_to_all x2 -> x0, waiting for transfers between devices: 10.1 us -> none  [the longest x1 10.1 us: per_device(): lax.all_to_all(cache_out, 'seq', split_axis=0, concat_axis=0, tiled=True)]
    all_to_all x2 -> x0, starting transfers between devices: 7.63 us -> none  [the longest x1 4.12 us: per_device(): lax.all_to_all(cache_out, 'seq', split_axis=0, concat_axis=0, tiled=True)]
  transfers between devices with their start and end apart: 4 -> 0, of which waited for: 2 -> 0; matrix products, arithmetic and copies ran while one was open for 32% -> 0% of each run, Pallas kernels for 0% -> 0%
where the time goes in v1:
time: 50.9 us; the launch traced here: 50.6 us
  Pallas kernels  47.7 us (94%)
  local copies, waits for them, and re-layouts  2.88 us (6%)
    pallas_call x1, Pallas kernels, per_device(): pl.pallas_call(functools.partial(kernel, (S, H, R, LR, KVH, G, LC)), out_...  47.7 us
    unnamed x1, local copies, waits for them, and re-layouts  1.57 us
    reshape x1, local copies, waits for them, and re-layouts, per_device(): norm_gain.reshape(1, M)  1.31 us

profile of v1, /device:TPU:0, one launch (start us, length us, event | category | flops | bytes accessed | tf_op | source)
XLA Modules:
  0.0 50.6 jit_solution(17861643137064839749)
XLA Ops:
  0.0 1.3 %reshape.3.gain_ref = bf16[1,4096]{1,0:T(2,128)(2,1)} reshape(bf16[4096]{0:T(1024)(128)(2,1)} %param.12) | data formatting | bytes 16384 | tf_op jit(solution)/shard_map/reshape | solution.py:412
  1.3 47.7 %shard_map.109 = bf16[64,1024]{1,0:T(8,128)(2,1)} custom-call(s32[8]{0:T(128)} %len_ref.1, s32[8,16]{1,0:T(8,128)} %slot_ref.1, s32[8,64]{1,0:T(8,128)} %parents_ref.1, bf16[1,4096]{1,0:T(2,128)(2,1)} %reshape.3.gain_ref, bf16[64,4096]{1,0:T(8,128)(2,1)} %tok_hbm.1, bf16[4096,1024]{1,0:T(8,128)(2,1)} %wq_hbm.1, bf16[4096,256]{1,0:T(8,128)(2,1)} %wk_hbm.1, ...), custom_call_target="tpu_custom_call" | custom-call | tf_op jit(solution)/shard_map/pallas_call | solution.py:366
  49.0 1.6 %copy.13 = bf16[64,1024]{1,0:T(8,128)(2,1)} copy(bf16[64,1024]{1,0:T(8,128)(2,1)} %shard_map.109) | data formatting | bytes 262144

commit v2 on v1

--- a/solution.py
+++ b/solution.py
@@ -10,6 +10,7 @@
 HEAD_WIDTH = 128
 TQ = 64
 BLK = 128
+KEYS_AT_ONCE = 512
 
 norm_epsilon = 1e-05
 masked_score = -1e30
@@ -114,11 +115,9 @@
         )
 
     def device_at(i):
-        same = xor(chip, i - 1, nch) * 2 + core
-        other = xor(chip, 2 * nch - i, nch) * 2 + (1 - core)
-        dev = jnp.where(i <= nch, same, other)
-        dev = jnp.where(i == 1, partner, dev)
-        return jnp.where(i == 0, me, dev)
+        same = xor(chip, i, nch) * 2 + core
+        other = xor(chip, 2 * nch - 1 - i, nch) * 2 + (1 - core)
+        return jnp.where(i < nch, same, other)
 
     tok_copy = pltpu.make_async_copy(tok_hbm, tok, tok_sem)
     tok_copy.start()
@@ -164,12 +163,21 @@
     normed = (
         inputs
         * lax.rsqrt(jnp.mean(inputs * inputs, axis=-1, keepdims=True) + norm_epsilon)
-        * gain_ref[...].astype(f32)
+        * gain_ref[...].astype(f32).reshape(1, -1)
     ).astype(bf16)
 
+    q_copies = []
     for c in range(KVH):
         wq_copies[c].wait()
         q_all[me, c] = jnp.dot(normed, wq[c], preferred_element_type=f32).astype(bf16)
+        if c == 0:
+            pl.semaphore_wait(barrier, S - 1 + H - 1)
+        for i in range(nch):
+            to = partner if i == 0 else xor(chip, i, nch) * 2 + core
+            q_copies.append(
+                remote(q_all.at[me, c], q_all.at[me, c], q_send.at[i, c], q_recv.at[me, c], seq=to)
+            )
+            q_copies[-1].start()
         if c == 0:
             def load(i, carry):
                 r = device_at(i) if group == 1 else i
@@ -182,15 +190,6 @@
                 pltpu.make_async_copy(
                     wo_hbm.at[:, h * W : (h + 1) * W], wo.at[h], wo_sem.at[h]
                 ).start()
-
-    pl.semaphore_wait(barrier, S - 1 + H - 1)
-    q_copies = []
-    for i in range(1, nch + 1):
-        to = partner if i == 1 else xor(chip, i - 1, nch) * 2 + core
-        q_copies.append(
-            remote(q_all.at[me], q_all.at[me], q_send.at[i], q_recv.at[me], seq=to)
-        )
-        q_copies[-1].start()
 
     slot = me % group
     for which in range(2):
@@ -247,13 +246,14 @@
 
         @pl.when(i > 0)
         def _():
-            remote(q_all.at[dev], q_all.at[dev], q_send.at[0], q_recv.at[dev]).wait_recv()
-
-        @pl.when((i > 1) & (i <= nch))
+            for c in range(KVH):
+                remote(q_all.at[dev, c], q_all.at[dev, c], q_send.at[0, c], q_recv.at[dev, c]).wait_recv()
+
+        @pl.when((i > 0) & (i < nch))
         def _():
-            remote(
-                q_all.at[dev], q_all.at[dev], f_send.at[i], q_recv.at[dev], seq=partner
-            ).start()
+            for c in range(KVH):
+                block = q_all.at[dev, c]
+                remote(block, block, f_send.at[i, c], q_recv.at[dev, c], seq=partner).start()
 
         if group == 1:
             pltpu.make_async_copy(k_hbm.at[r], kbuf.at[r], k_sem.at[r]).wait()
@@ -262,14 +262,22 @@
         cols = []
         for h in range(KVH):
             q = stacked(q_all[dev, h])
-            keys = kbuf[r, :, h * D : (h + 1) * D]
-            vals = vbuf[r, :, h * D : (h + 1) * D]
-            s = lax.dot_general(q, keys, (((1,), (1,)), ((), ())), preferred_element_type=f32)
-            s = s + hidden
-            m = jnp.max(s, axis=-1, keepdims=True)
-            p = jnp.exp2((s - m) * exp2_scale)
-            total = jnp.maximum(jnp.sum(p, axis=-1, keepdims=True), 1.0)
-            o = jnp.dot(p.astype(bf16), vals, preferred_element_type=f32)
+            cuts = [slice(at, at + KEYS_AT_ONCE) for at in range(0, LC, KEYS_AT_ONCE)]
+            parts = []
+            for cut in cuts:
+                keys = kbuf[r, cut, h * D : (h + 1) * D]
+                s = lax.dot_general(q, keys, (((1,), (1,)), ((), ())), preferred_element_type=f32)
+                parts.append(s + hidden[:, cut])
+            m = functools.reduce(
+                jnp.maximum, [jnp.max(s, axis=-1, keepdims=True) for s in parts]
+            )
+            total, o = 0.0, 0.0
+            for cut, s in zip(cuts, parts):
+                p = jnp.exp2((s - m) * exp2_scale)
+                total = total + jnp.sum(p, axis=-1, keepdims=True)
+                vals = vbuf[r, cut, h * D : (h + 1) * D]
+                o = o + jnp.dot(p.astype(bf16), vals, preferred_element_type=f32)
+            total = jnp.maximum(total, 1.0)
             o = (o / total).astype(bf16)
             lse = m * scale + jnp.log(total)
             for g in range(G):
@@ -289,8 +297,10 @@
 
     for copy in q_copies:
         copy.wait_send()
-    for i in range(2, nch + 1):
-        remote(q_all.at[me], q_all.at[me], f_send.at[i], q_recv.at[me]).wait_send()
+    for i in range(1, nch):
+        for c in range(KVH):
+            block = q_all.at[me, c]
+            remote(block, block, f_send.at[i, c], q_recv.at[me, c]).wait_send()
     orecv[me] = osend[me]
     lrecv[me] = lsend[me]
 
@@ -393,9 +403,9 @@
                 dma((H,)),
                 dma((R,)),
                 dma((R,)),
-                dma((S,)),
-                dma((S,)),
-                dma((S,)),
+                dma((S, KVH)),
+                dma((S, KVH)),
+                dma((S, KVH)),
                 dma((S,)),
                 dma((S,)),
                 dma((S,)),
@@ -409,7 +419,7 @@
                 collective_id=0, has_side_effects=True, vmem_limit_bytes=66 * 1000 * 1000
             ),
         )(
-            lengths, slot_block, parents, norm_gain.reshape(1, M), tokens,
+            lengths, slot_block, parents, norm_gain, tokens,
             w_query, key_projection, value_projection, w_out, cache_keys, paged_value_cache,
         )
 

time: 50.9 us -> 47.4 us (0.931)
  Pallas kernels: 47.7 us -> 45.6 us
  local copies, waits for them, and re-layouts: 2.88 us -> 1.57 us
    pallas_call x1, Pallas kernels: 47.7 us -> 45.6 us  [per_device(): pl.pallas_call(functools.partial(kernel, (S, H, R, LR, KVH, G, LC)), out_...]
    reshape x1 -> x0, local copies, waits for them, and re-layouts: 1.31 us -> none  [per_device(): norm_gain.reshape(1, M)]
where the time goes in v2:
time: 47.4 us; the launch traced here: 47.2 us
  Pallas kernels  45.6 us (96%)
  local copies, waits for them, and re-layouts  1.57 us (3%)
    pallas_call x1, Pallas kernels, per_device(): pl.pallas_call(functools.partial(kernel, (S, H, R, LR, KVH, G, LC)), out_...  45.6 us
    unnamed x1, local copies, waits for them, and re-layouts  1.57 us

profile of v2, /device:TPU:0, one launch (start us, length us, event | category | flops | bytes accessed | tf_op | source)
XLA Modules:
  0.0 47.2 jit_solution(4980576833373411584)
XLA Ops:
  0.0 45.6 %shard_map.109 = bf16[64,1024]{1,0:T(8,128)(2,1)} custom-call(s32[8]{0:T(128)} %len_ref.1, s32[8,16]{1,0:T(8,128)} %slot_ref.1, s32[8,64]{1,0:T(8,128)} %parents_ref.1, bf16[4096]{0:T(1024)(128)(2,1)} %gain_ref.1, bf16[64,4096]{1,0:T(8,128)(2,1)} %tok_hbm.1, bf16[4096,1024]{1,0:T(8,128)(2,1)} %wq_hbm.1, bf16[4096,256]{1,0:T(8,128)(2,1)} %wk_hbm.1, ...), custom_call_target="tpu_custom_call" | custom-call | tf_op jit(solution)/shard_map/pallas_call | solution.py:376
  45.6 1.6 %copy.13 = bf16[64,1024]{1,0:T(8,128)(2,1)} copy(bf16[64,1024]{1,0:T(8,128)(2,1)} %shard_map.109) | data formatting | bytes 262144
